TPU v7x, 128 devices: a whole 4x4x4 slice. The times are simulated.
128 devices in a mesh: gx: 4 (over z), gy: 16 (over y, x), gz: 2 (over core).
Axes of the slice: x: 4, y: 4, z: 4, core: 2. Of those that a mesh axis runs over, the one named last changes fastest.
Arguments:
- particles: float32 [8, 1048576], P(None, ('gx', 'gy', 'gz')), may hold values from -0.5 to 0.5
- dest_key: int32 [1048576], P(('gx', 'gy', 'gz')), may hold values from 0 to 127, as said below
- cell_a: int32 [1048576], P(('gx', 'gy', 'gz')), may hold values from 0 to 255
- cell_b: int32 [1048576], P(('gx', 'gy', 'gz')), may hold values from 0 to 127
- velocity: float32 [2, 1024, 4096], P(None, 'gx', ('gy', 'gz')), may hold values from -6 to 6
Outputs:
- binned: float32 [8, 4194304], P(None, ('gx', 'gy', 'gz'))
- binned_cell: int32 [4194304], P(('gx', 'gy', 'gz'))
Inputs may be any that keep to these rules, and one draw needn't show every extreme that they name: Of the particles of one device at most 256 have any one value of dest_key, and one device is named by exactly 256 particles of every device.
All inputs are finite; a program needn't handle non-finite values.
Results may differ from a plain program's by a relative error of at most 0.0003.
Values sent between devices are 32-bit elements; how exact they have to be, the bound alone decides.
A program may use at most 64 MiB of HBM per device.

v0:
```python
import functools

import jax
import jax.numpy as jnp
from jax import lax
from jax.experimental import pallas as pl
from jax.experimental.pallas import tpu as pltpu
from jax.sharding import PartitionSpec as P

step_length = 0.5
NT = (((1,), (1,)), ((), ()))


def quad_weights(frac):
    return (0.5 * frac * (frac - 1.0), 1.0 - frac * frac, 0.5 * frac * (frac + 1.0))


def rounded(x):
    return x.astype(jnp.bfloat16).astype(jnp.float32)


def pack_edges(vel_ref, edge_ref):
    tile_height, tile_width = vel_ref.shape[1:]
    edge_ref[...] = jnp.zeros_like(edge_ref)
    for c in range(2):
        edge_ref[4 * c:4 * c + 1, :tile_width] = vel_ref[c, 0:1, :]
        edge_ref[4 * c + 1:4 * c + 2, :tile_width] = vel_ref[c, tile_height - 1:, :]
        turned = jnp.transpose(vel_ref[c])
        edge_ref[4 * c + 2:4 * c + 3, :tile_height] = turned[0:1]
        edge_ref[4 * c + 3:4 * c + 4, :tile_height] = turned[tile_width - 1:]


def rank_particles(owners, cap, chunk, block, key_ref, seen_ref, hot_ref):
    count = key_ref.shape[1]
    seen_ref[...] = jnp.zeros_like(seen_ref)
    upper = (lax.broadcasted_iota(jnp.int32, (block, block), 0)
             < lax.broadcasted_iota(jnp.int32, (block, block), 1)).astype(jnp.float32).astype(jnp.bfloat16)
    owner_ids = lax.broadcasted_iota(jnp.int32, (owners, block), 0)
    rank_ids = lax.broadcasted_iota(jnp.int32, (cap, block), 0)

    def one_chunk(index, carry):
        for part in range(chunk // block):
            start = pl.multiple_of(index * chunk + part * block, block)
            keys = key_ref[:, pl.ds(start, block)]
            hot = (owner_ids == keys).astype(jnp.float32)
            before = jnp.dot(hot.astype(jnp.bfloat16), upper, preferred_element_type=jnp.float32)
            seen = seen_ref[...]
            ranks = jnp.sum(hot * (before + seen[:, :1]), axis=0, keepdims=True).astype(jnp.int32)
            seen_ref[...] = seen + jnp.sum(hot, axis=1, keepdims=True)
            hot_ref[:, pl.ds(start, block)] = (rank_ids == ranks).astype(jnp.float32).astype(jnp.bfloat16)
        return carry

    lax.fori_loop(0, count // chunk, one_chunk, 0)


def place_group(ids, cap, tile_width, chunk, block, part_ref, key_ref, a_ref, b_ref,
                hot_ref, pick_ref, acc_ref, outs):
    count = key_ref.shape[1]
    group = len(ids)
    acc_ref[...] = jnp.zeros_like(acc_ref)
    row = lax.broadcasted_iota(jnp.int32, (group, block), 0)
    wanted = jnp.zeros((group, block), jnp.int32)
    for i, owner in enumerate(ids):
        wanted = jnp.where(row == i, owner, wanted)

    def one_chunk(index, carry):
        for part in range(chunk // block):
            start = pl.multiple_of(index * chunk + part * block, block)
            at = slice(part * block, (part + 1) * block)
            keys = key_ref[:, pl.ds(start, block)]
            values = part_ref[:, pl.ds(start, block)]
            high = rounded(values)
            both = jnp.concatenate([high, values - high], axis=0)
            for i, owner in enumerate(ids):
                pick_ref[i * 16:(i + 1) * 16, at] = jnp.where(
                    keys == owner, both, 0.0).astype(jnp.bfloat16)
            hot = wanted == keys
            rows = (a_ref[:, pl.ds(start, block)] + 1).astype(jnp.float32)
            cols = b_ref[:, pl.ds(start, block)].astype(jnp.float32)
            pick_ref[group * 16:group * 17, at] = jnp.where(hot, rows, 0.0).astype(jnp.bfloat16)
            pick_ref[group * 17:group * 18, at] = jnp.where(hot, cols, 0.0).astype(jnp.bfloat16)
        columns = pl.ds(pl.multiple_of(index * chunk, chunk), chunk)
        acc_ref[...] += lax.dot_general(pick_ref[...], hot_ref[:, columns], NT,
                                        preferred_element_type=jnp.float32)
        return carry

    lax.fori_loop(0, count // chunk, one_chunk, 0)
    cells = (acc_ref[group * 16:group * 17, :] * float(tile_width)
             + acc_ref[group * 17:group * 18, :] - float(tile_width))
    for i, out in enumerate(outs):
        low = i * 16
        out[:, :cap] = acc_ref[low:low + 8, :] + acc_ref[low + 8:low + 16, :]
        for j in range(cap // 128):
            out[j:j + 1, cap:] = cells[i:i + 1, j * 128:(j + 1) * 128]
        if cap // 128 < 8:
            out[cap // 128:, cap:] = jnp.zeros((8 - cap // 128, 128), jnp.float32)


def banded(node, index, weights):
    diff = node - index
    masks = [diff == shift for shift in (-1, 0, 1)]
    return [jnp.where(masks[0], w[0], jnp.where(masks[1], w[1], jnp.where(masks[2], w[2], jnp.zeros_like(w[2]))))
            for w in weights]


def advance(block, cap, tile_height, tile_width, lhs_ref, piece):
    values = block[:, :cap]
    cells = jnp.concatenate([block[j:j + 1, cap:] for j in range(cap // 128)], axis=1)
    cells = cells.astype(jnp.int32)
    rows_out, cells_out = [], []
    width = lhs_ref.shape[0] // 2
    depth = 3 * tile_height + 16
    row_node = lax.broadcasted_iota(jnp.int32, (tile_height, piece), 0).astype(jnp.float32).astype(jnp.bfloat16)
    col_node = lax.broadcasted_iota(jnp.int32, (width, piece), 0)
    col_node = jnp.where(col_node < tile_width, col_node, jnp.where(
        col_node == tile_width, -1, jnp.where(col_node == tile_width + 1, tile_width, -5)))
    spare = lax.broadcasted_iota(jnp.int32, (16, piece), 0)
    for start in range(0, cap, piece):
        v = values[:, start:start + piece]
        cell = cells[:, start:start + piece]
        live = cell >= 0
        safe = jnp.maximum(cell, 0)
        node_row = safe // tile_width
        node_col = safe - node_row * tile_width
        wa = quad_weights(v[0:1])
        wb = quad_weights(v[1:2])
        high = [rounded(w) for w in wa]
        low = [w - h for w, h in zip(wa, high)]
        narrow = [[w.astype(jnp.bfloat16) for w in ws] for ws in (high, low)]
        w_high, w_low = banded(row_node, node_row.astype(jnp.float32).astype(jnp.bfloat16), narrow)
        above, below = node_row == 0, node_row == tile_height - 1
        edge = jnp.where(
            spare < 4,
            jnp.where(spare % 2 == 0, jnp.where(above, high[0], 0.0), jnp.where(below, high[2], 0.0)),
            jnp.where(spare == 4, jnp.where(above, low[0], 0.0),
                      jnp.where(spare == 5, jnp.where(below, low[2], 0.0), 0.0)))
        mixed = jnp.dot(lhs_ref[:, :depth],
                        jnp.concatenate([w_high, w_high, w_low, edge.astype(jnp.bfloat16)], axis=0),
                        preferred_element_type=jnp.float32)
        (col_weight,) = banded(col_node, node_col, (wb,))
        scale = jnp.where(live, step_length, 0.0)
        first = jnp.sum(mixed[:width] * col_weight, axis=0, keepdims=True) * scale
        second = jnp.sum(mixed[width:] * col_weight, axis=0, keepdims=True) * scale
        row = lax.broadcasted_iota(jnp.int32, v.shape, 0)
        rows_out.append(v + jnp.where(row == 2, first, jnp.where(row == 3, second, 0.0)))
        cells_out.append(jnp.where(live, cell, -1))
    return rows_out, cells_out


DIRS = ((-1, -1), (-1, 0), (-1, 1), (0, -1), (0, 1), (1, -1), (1, 0), (1, 1))


def build_lhs(vel_ref, halo_ref, lhs_ref, tile_height, tile_width):
    width = lhs_ref.shape[0] // 2
    lane = lax.broadcasted_iota(jnp.int32, (1, 128), 1)

    def beside(da, db, row):
        return halo_ref[DIRS.index((da, db)), row:row + 1, :]

    for c in range(2):
        own = jnp.transpose(vel_ref[c])
        left = beside(0, -1, 4 * c + 3)[:, :tile_height]
        right = beside(0, 1, 4 * c + 2)[:, :tile_height]
        rest = jnp.zeros((width - tile_width - 2, tile_height), jnp.float32)
        body = jnp.concatenate([own, left, right, rest], axis=0)
        high = rounded(body)
        low = body - high

        def outer(da, row):
            middle = beside(da, 0, row)[:, :tile_width]
            west = beside(da, -1, row)[:, tile_width - 1:tile_width]
            east = beside(da, 1, row)[:, 0:1]
            return jnp.concatenate(
                [middle, jnp.where(lane == 0, west, jnp.where(lane == 1, east, 0.0))], axis=1)

        ends = jnp.concatenate([outer(-1, 4 * c + 1), outer(1, 4 * c)], axis=0)
        ends_high = rounded(ends)
        extra = jnp.concatenate([ends_high, ends - ends_high, ends_high], axis=0)
        extra = jnp.concatenate([extra, jnp.zeros((122, extra.shape[1]), jnp.float32)], axis=0)
        extra = jnp.transpose(extra)[:width]
        lhs_ref[c * width:(c + 1) * width, :] = jnp.concatenate(
            [high, low, high, extra], axis=1).astype(jnp.bfloat16)


def exchange_kernel(sizes, cap, piece, groups, chunk, block, part_ref, key_ref, a_ref, b_ref, vel_ref,
                    out_ref, cell_ref, outgoing, edge_ref, seen_ref, hot_ref, pick_ref, acc_ref,
                    held, halo_ref, lhs_ref, send_sem, recv_sem, halo_send, halo_recv):
    nx, ny, nz = sizes
    plane = ny * nz
    n = nx * plane
    tile_height, tile_width = vel_ref.shape[1:]
    gx, gy, gz = lax.axis_index("gx"), lax.axis_index("gy"), lax.axis_index("gz")
    column = gy * nz + gz

    def at(dx, dyz, sign):
        x = lax.rem(gx + sign * dx + nx, nx)
        y = lax.rem(gy + sign * (dyz // nz) + ny, ny)
        z = lax.rem(gz + sign * lax.rem(dyz, nz) + nz, nz)
        return x, y, z

    def linear(place):
        return (place[0] * ny + place[1]) * nz + place[2]

    def halo_copy(k):
        da, db = DIRS[k]
        there = column + db
        return pltpu.make_async_remote_copy(
            src_ref=edge_ref, dst_ref=halo_ref.at[7 - k], send_sem=halo_send.at[k],
            recv_sem=halo_recv.at[7 - k], device_id=(gx + da, there // nz, lax.rem(there, nz)),
            device_id_type=pl.DeviceIdType.MESH)

    def halo_arrival(k):
        da, db = DIRS[k]
        there = column + db
        return pltpu.make_async_remote_copy(
            src_ref=edge_ref, dst_ref=halo_ref.at[k], send_sem=halo_send.at[k],
            recv_sem=halo_recv.at[k], device_id=(gx + da, there // nz, lax.rem(there, nz)),
            device_id_type=pl.DeviceIdType.MESH)

    def exists(k):
        da, db = DIRS[k]
        a, b = gx + da, column + db
        return (a >= 0) & (a < nx) & (b >= 0) & (b < plane)

    def block_copy(dx, dyz):
        target = at(dx, dyz, 1)
        slot = dx * plane + dyz
        return pltpu.make_async_remote_copy(
            src_ref=outgoing.at[slot], dst_ref=held.at[slot],
            send_sem=send_sem.at[slot], recv_sem=recv_sem.at[slot], device_id=target,
            device_id_type=pl.DeviceIdType.MESH)

    pack_edges(vel_ref, edge_ref)
    rank_particles(n, cap, chunk, block, key_ref, seen_ref, hot_ref)
    for k in range(8):
        @pl.when(exists(k))
        def _(k=k):
            halo_copy(k).start()

        @pl.when(jnp.logical_not(exists(k)))
        def _(k=k):
            halo_ref[k] = jnp.zeros(halo_ref.shape[1:], jnp.float32)

    share = n // groups
    for g in range(groups):
        ids, outs = [], []
        for q in range(g * share, (g + 1) * share):
            dx, dyz = q % nx, q // nx
            ids.append(linear(at(dx, dyz, 1)))
            outs.append(held.at[0] if q == 0 else outgoing.at[dx * plane + dyz])
        place_group(ids, cap, tile_width, chunk, block, part_ref, key_ref, a_ref, b_ref,
                    hot_ref, pick_ref, acc_ref, outs)
        for q in range(max(1, g * share), (g + 1) * share):
            block_copy(q % nx, q // nx).start()

    for k in range(8):
        @pl.when(exists(k))
        def _(k=k):
            halo_arrival(k).wait_recv()

    build_lhs(vel_ref, halo_ref, lhs_ref, tile_height, tile_width)

    def work(dx, dyz):
        slot = dx * plane + dyz
        source = linear(at(dx, dyz, -1))
        rows_out, cells_out = advance(held[slot], cap, tile_height, tile_width, lhs_ref, piece)
        for k, start in enumerate(range(0, cap, piece)):
            spot = pl.ds(pl.multiple_of(source * cap + start, 128), piece)
            out_ref[:, spot] = rows_out[k]
            cell_ref[:, spot] = cells_out[k]

    def one(q, carry):
        near = q < plane
        r = jnp.maximum(q - plane, 0)
        dx = jnp.where(near, 0, lax.rem(r, nx - 1) + 1)
        dyz = jnp.where(near, q, r // (nx - 1))

        @pl.when(q > 0)
        def _():
            block_copy(dx, dyz).wait_recv()

        work(dx, dyz)
        return carry

    lax.fori_loop(0, n, one, 0)

    def sent(q, carry):
        block_copy(lax.rem(q, nx), q // nx).wait_send()
        return carry

    lax.fori_loop(1, n, sent, 0)
    for k in range(8):
        @pl.when(exists(k))
        def _(k=k):
            halo_copy(k).wait_send()


def shards(particles, dest_key, cell_a, cell_b, velocity):
    owners = lax.axis_size(("gx", "gy", "gz"))
    count = particles.shape[1]
    cap = 4 * count // owners
    tile_height, tile_width = velocity.shape[1:]
    assert tile_height <= 256 and tile_width <= 256 and cap % 128 == 0 and cap <= 1024
    chunk, block, groups = 1024, 256, 2
    reach = max(tile_height, tile_width)
    piece = min(cap, 256)
    width = -(-(tile_width + 2) // 8) * 8
    sizes = tuple(lax.axis_size(name) for name in ("gx", "gy", "gz"))
    picks = owners // groups * 18
    binned, binned_cell = pl.pallas_call(
        functools.partial(exchange_kernel, sizes, cap, piece, groups, chunk, block),
        out_shape=(jax.ShapeDtypeStruct((8, owners * cap), jnp.float32),
                   jax.ShapeDtypeStruct((1, owners * cap), jnp.int32)),
        in_specs=[pl.BlockSpec(memory_space=pltpu.VMEM)] * 5,
        out_specs=(pl.BlockSpec(memory_space=pltpu.VMEM),) * 2,
        scratch_shapes=[
            pltpu.VMEM((owners, 8, cap + 128), jnp.float32),
            pltpu.VMEM((8, reach), jnp.float32),
            pltpu.VMEM((owners, 128), jnp.float32),
            pltpu.VMEM((cap, count), jnp.bfloat16),
            pltpu.VMEM((picks, chunk), jnp.bfloat16),
            pltpu.VMEM((picks, cap), jnp.float32),
            pltpu.VMEM((owners, 8, cap + 128), jnp.float32),
            pltpu.VMEM((8, 8, reach), jnp.float32),
            pltpu.VMEM((2 * width, 3 * tile_height + 128), jnp.bfloat16),
            pltpu.SemaphoreType.DMA((owners,)),
            pltpu.SemaphoreType.DMA((owners,)),
            pltpu.SemaphoreType.DMA((8,)),
            pltpu.SemaphoreType.DMA((8,)),
        ],
        compiler_params=pltpu.CompilerParams(has_side_effects=True),
    )(particles, dest_key.reshape(1, -1), cell_a.reshape(1, -1), cell_b.reshape(1, -1), velocity)
    return (binned, binned_cell.reshape(-1))


def solution(mesh):
    in_specs = (
        P(None, ("gx", "gy", "gz")),
        P(("gx", "gy", "gz")),
        P(("gx", "gy", "gz")),
        P(("gx", "gy", "gz")),
        P(None, "gx", ("gy", "gz")),
    )
    out_specs = (P(None, ("gx", "gy", "gz")), P(("gx", "gy", "gz")))
    return jax.shard_map(shards, mesh=mesh, in_specs=in_specs, out_specs=out_specs, check_vma=False)
```

profile of v0, /device:TPU:1, one launch (start us, length us, event | category | flops | bytes accessed | tf_op | source)
XLA Modules:
  0.0 95.2 jit_solution(15985928263144467465)
XLA Ops:
  0.6 91.6 %shard_map.68 = (f32[8,32768]{1,0:T(8,128)}, s32[1,32768]{1,0:T(1,128)}) custom-call(f32[8,8192]{1,0:T(8,128)} %part_ref.1, s32[1,8192]{1,0:T(1,128)} %bitcast.5, s32[1,8192]{1,0:T(1,128)} %bitcast.6, s32[1,8192]{1,0:T(1,128)} %bitcast.7, f32[2,256,128]{2,1,0:T(8,128)} %vel_ref.1), custom_call_target="tpu_custom_call" | custom-call | tf_op jit(solution)/shard_map/pallas_call | solution.py:310
  92.3 0.0 copy-start
  92.3 2.3 %copy.9 = f32[8,32768]{1,0:T(8,128)} copy(f32[8,32768]{1,0:T(8,128)} %get-tuple-element.8) | data formatting | bytes 2097152
  94.6 0.0 copy-done
  94.6 0.7 copy.10
Async XLA Ops:
  92.3 2.3 %copy-start = (s32[1,32768]{1,0:T(1,128)S(1)}, s32[1,32768]{1,0:T(1,128)}, u32[]{:S(2)}) copy-start(s32[1,32768]{1,0:T(1,128)} %get-tuple-element.5) | copy-start | bytes 393220
where the time goes:
time: 96.5 us; the launch traced here: 95.2 us
  Pallas kernels  91.6 us (95%)
  local copies, waits for them, and re-layouts  2.97 us (3%)
    pallas_call x1, Pallas kernels, shards(): pl.pallas_call(functools.partial(exchange_kernel, sizes, cap, piece, grou...  91.6 us
    unnamed x4, local copies, waits for them, and re-layouts  2.97 us

commit v1 on v0

v1 whole, which is shorter than its diff:
```python
import functools

import jax
import jax.numpy as jnp
from jax import lax
from jax.experimental import pallas as pl
from jax.experimental.pallas import tpu as pltpu
from jax.sharding import PartitionSpec as P

step_length = 0.5
NT = (((1,), (1,)), ((), ()))
LANES = 128
BLOCK_A, BLOCK_B = 4, 32
DIRS = ((-1, -1), (-1, 0), (-1, 1), (0, -1), (0, 1), (1, -1), (1, 0), (1, 1))


def quad_weights(frac):
    return (0.5 * frac * (frac - 1.0), 1.0 - frac * frac, 0.5 * frac * (frac + 1.0))


def rounded(x):
    return x.astype(jnp.bfloat16).astype(jnp.float32)


def narrow_iota(shape, dim):
    return lax.broadcasted_iota(jnp.int32, shape, dim).astype(jnp.float32).astype(jnp.bfloat16)


def one_hot(row, index):
    one, zero = jnp.ones((), jnp.bfloat16), jnp.zeros((), jnp.bfloat16)
    return jnp.where(row == index, one, zero)


def pack_edges(vel_ref, edge_ref):
    tile_height, tile_width = vel_ref.shape[1:]
    edge_ref[...] = jnp.zeros_like(edge_ref)
    for c in range(2):
        edge_ref[4 * c:4 * c + 1, :tile_width] = vel_ref[c, 0:1, :]
        edge_ref[4 * c + 1:4 * c + 2, :tile_width] = vel_ref[c, tile_height - 1:, :]
        turned = jnp.transpose(vel_ref[c])
        edge_ref[4 * c + 2:4 * c + 3, :tile_height] = turned[0:1]
        edge_ref[4 * c + 3:4 * c + 4, :tile_height] = turned[tile_width - 1:]


def sort_particles(owners, width, chunk, part_ref, key_ref, a_ref, b_ref,
                   hot_ref, base_ref, pick_ref, low_ref, acc_ref, sorted_ref, cells_ref, table_ref):
    count = key_ref.shape[1]
    owner_rows = narrow_iota((owners, width), 0)
    ones = jnp.ones((width, LANES), jnp.bfloat16)
    base_ref[...] = jnp.zeros_like(base_ref)
    tops = count // width

    def count_chunk(index, seen):
        for part in range(chunk // width):
            start = pl.multiple_of(index * chunk + part * width, width)
            keys = key_ref[:, pl.ds(start, width)].astype(jnp.float32).astype(jnp.bfloat16)
            hot = one_hot(owner_rows, keys)
            hot_ref[:, pl.ds(start, width)] = hot
            base_ref[index * (chunk // width) + part] = seen
            seen = seen + jnp.dot(hot, ones, preferred_element_type=jnp.float32)
        return seen

    total = lax.fori_loop(0, count // chunk, count_chunk, jnp.zeros((owners, LANES), jnp.float32))
    below = (lax.broadcasted_iota(jnp.int32, (owners, owners), 1)
             < lax.broadcasted_iota(jnp.int32, (owners, owners), 0)).astype(jnp.float32).astype(jnp.bfloat16)
    first = jnp.dot(below, total.astype(jnp.bfloat16), preferred_element_type=jnp.float32)
    eye = (lax.broadcasted_iota(jnp.int32, (owners, LANES), 1)
           == lax.broadcasted_iota(jnp.int32, (owners, LANES), 0))
    firsts = jnp.sum(jnp.where(eye, first, 0.0), axis=0, keepdims=True)
    totals = jnp.sum(jnp.where(eye, total, 0.0), axis=0, keepdims=True)
    table_ref[0:1, :] = firsts.astype(jnp.int32)
    table_ref[1:2, :] = totals.astype(jnp.int32)

    upper = (lax.broadcasted_iota(jnp.int32, (width, width), 0)
             < lax.broadcasted_iota(jnp.int32, (width, width), 1)).astype(jnp.float32).astype(jnp.bfloat16)
    owner_ids = lax.broadcasted_iota(jnp.int32, (owners, LANES), 0)
    low_rows = narrow_iota((width, width), 0)
    top_rows = narrow_iota((tops, width), 0)
    zero = jnp.zeros((), jnp.bfloat16)

    acc_ref[...] = jnp.zeros_like(acc_ref)

    def place_chunk(index, carry):
        for part in range(chunk // width):
            start = pl.multiple_of(index * chunk + part * width, width)
            at = slice(part * width, (part + 1) * width)
            before = jnp.dot(hot_ref[:, pl.ds(start, width)], upper, preferred_element_type=jnp.float32)
            base = base_ref[index * (chunk // width) + part] + first
            keys = key_ref[:, pl.ds(start, width)]
            spots = []
            for j in range(width // LANES):
                cut = slice(j * LANES, (j + 1) * LANES)
                spots.append(jnp.sum(jnp.where(owner_ids == keys[:, cut], before[:, cut] + base, 0.0),
                                     axis=0, keepdims=True))
            spot = jnp.concatenate(spots, axis=1).astype(jnp.int32)
            top_int = spot // width
            top = top_int.astype(jnp.float32).astype(jnp.bfloat16)
            low = (spot - top_int * width).astype(jnp.float32).astype(jnp.bfloat16)
            low_ref[:, at] = one_hot(low_rows, low)
            values = part_ref[:, pl.ds(start, width)]
            high = rounded(values)
            both = jnp.concatenate([high, values - high], axis=0).astype(jnp.bfloat16)
            for i in range(tops):
                pick_ref[i * 16:(i + 1) * 16, at] = jnp.where(top == jnp.full((), i, jnp.bfloat16), both, zero)
            rows = a_ref[:, pl.ds(start, width)].astype(jnp.float32).astype(jnp.bfloat16)
            cols = b_ref[:, pl.ds(start, width)].astype(jnp.float32).astype(jnp.bfloat16)
            mine = top_rows == top
            pick_ref[tops * 16:tops * 17, at] = jnp.where(mine, rows, zero)
            pick_ref[tops * 17:tops * 18, at] = jnp.where(mine, cols, zero)
        acc_ref[...] += lax.dot_general(pick_ref[...], low_ref[...], NT, preferred_element_type=jnp.float32)
        return carry

    lax.fori_loop(0, count // chunk, place_chunk, 0)


def unpack_sorted(tops, width, tile_width, acc_ref, sorted_ref, cells_ref):
    cells = acc_ref[tops * 16:tops * 17, :] * float(tile_width) + acc_ref[tops * 17:tops * 18, :]
    for i in range(tops):
        at = slice(i * width, (i + 1) * width)
        sorted_ref[:, at] = acc_ref[i * 16:i * 16 + 8, :] + acc_ref[i * 16 + 8:i * 16 + 16, :]
        cells_ref[0:1, at] = cells[i:i + 1, :]


def cut_block(first, size, sorted_ref, cells_ref, out):
    base = pl.multiple_of((first // LANES) * LANES, LANES)
    shift = first - base
    back = lax.rem(LANES - shift, LANES)
    lane = lax.broadcasted_iota(jnp.int32, (8, LANES), 1)
    near = lane < LANES - shift
    for source, rows in ((sorted_ref, 8), (cells_ref, 1)):
        turned = [pltpu.roll(source[:, pl.ds(base + j * LANES, LANES)], back, 1) for j in range(3)]
        for j in range(2):
            piece = jnp.where(near, turned[j], turned[j + 1])
            if rows == 8:
                out[8 * j:8 * j + 8, :] = jnp.where(lane + j * LANES < size, piece, 0.0)
            else:
                out[16 + j:17 + j, :] = jnp.where(lane + j * LANES < size, piece, -1.0)[0:1]


def build_table(vel_ref, halo_ref, table_ref, tile_height, tile_width):
    width = tile_width + 8
    lane = lax.broadcasted_iota(jnp.int32, (1, LANES), 1)
    tall = tile_height // BLOCK_A
    wide = tile_width // BLOCK_B
    reach = BLOCK_A + 2
    node = lax.broadcasted_iota(jnp.int32, (tile_height + LANES, reach * tall), 0)
    slot = lax.broadcasted_iota(jnp.int32, (tile_height + LANES, reach * tall), 1)
    want = BLOCK_A * (slot % tall) + slot // tall - 1
    want = jnp.where(want < 0, tile_height, jnp.where(want == tile_height, tile_height + 1, want))
    select = (node == want).astype(jnp.float32).astype(jnp.bfloat16)

    def beside(da, db, row):
        return halo_ref[DIRS.index((da, db)), row:row + 1, :]

    for c in range(2):
        own = jnp.transpose(vel_ref[c])
        left = beside(0, -1, 4 * c + 3)[:, :tile_height]
        right = beside(0, 1, 4 * c + 2)[:, :tile_height]
        rest = jnp.zeros((width - tile_width - 2, tile_height), jnp.float32)
        body = jnp.concatenate([own, left, right, rest], axis=0)

        def outer(da, row):
            middle = beside(da, 0, row)[:, :tile_width]
            west = beside(da, -1, row)[:, tile_width - 1:tile_width]
            east = beside(da, 1, row)[:, 0:1]
            return jnp.concatenate(
                [middle, jnp.where(lane == 0, west, jnp.where(lane == 1, east, 0.0))], axis=1)

        ends = jnp.concatenate([outer(-1, 4 * c + 1), outer(1, 4 * c),
                                jnp.zeros((LANES - 2, 2 * LANES), jnp.float32)], axis=0)
        full = jnp.concatenate([body, jnp.transpose(ends)[:width]], axis=1)
        high = rounded(full)
        both = jnp.concatenate([high, full - high], axis=0).astype(jnp.bfloat16)
        spread = jnp.dot(both, select, preferred_element_type=jnp.float32)
        first_half = lax.broadcasted_iota(jnp.int32, (BLOCK_B, LANES), 1) < LANES // 2
        for part in range(2):
            z = spread[part * width:(part + 1) * width]
            plain = [z[:, j * LANES:(j + 1) * LANES] for j in range(reach * tall // LANES)]
            turned = [pltpu.roll(p, LANES // 2, 1) for p in plain]

            def joined(i, rows):
                j, half = i // 2, i % 2
                low, top = (plain[j], turned[j]) if half == 0 else (turned[j], plain[j])
                height = rows[0].stop - rows[0].start
                return jnp.concatenate([jnp.where(first_half[:height], low[rows[2 * k]], top[rows[2 * k + 1]])
                                        for k in range(wide // 2)], axis=1)

            columns = slice(part * tall * wide, (part + 1) * tall * wide)
            for i in range(reach):
                low = (c * reach + i) * BLOCK_B
                table_ref[low:low + BLOCK_B, columns] = joined(
                    i, [slice(BLOCK_B * k, BLOCK_B * (k + 1)) for k in range(wide)]).astype(jnp.bfloat16)
            for e in range(2):
                if e == 0:
                    lines = [tile_width] + [BLOCK_B * k - 1 for k in range(1, wide)]
                else:
                    lines = [BLOCK_B * (k + 1) for k in range(wide - 1)] + [tile_width + 1]
                rows = [joined(i, [slice(r, r + 1) for r in lines]) for i in range(reach)]
                rows.append(jnp.zeros((8 - reach, tall * wide), jnp.float32))
                low = 2 * reach * BLOCK_B + (c * 2 + e) * 8
                table_ref[low:low + 8, columns] = jnp.concatenate(rows, axis=0).astype(jnp.bfloat16)


def gather_nodes(blocks, tile_width, table_ref, nodes_ref):
    cells = jnp.concatenate([b[16 + j:17 + j, :] for b in blocks for j in range(2)], axis=1)
    cell = jnp.maximum(cells, 0.0).astype(jnp.int32)
    row = cell // tile_width
    col = cell - row * tile_width
    index = (col // BLOCK_B) * 64 + row // BLOCK_A
    index = index.astype(jnp.float32).astype(jnp.bfloat16)
    hot = one_hot(narrow_iota((256, index.shape[1]), 0), index)
    nodes_ref[...] = jnp.dot(table_ref[...], jnp.concatenate([hot, hot], axis=0),
                             preferred_element_type=jnp.float32)


def banded(diff, weights):
    return jnp.where(diff == -1, weights[0], jnp.where(diff == 0, weights[1], jnp.where(diff == 1, weights[2], 0.0)))


def weigh(v, cell, tile_width, nodes, weights_ref):
    reach = BLOCK_A + 2
    live = cell >= 0.0
    place = jnp.maximum(cell, 0.0).astype(jnp.int32)
    row = place // tile_width
    col = place - row * tile_width
    row = row % BLOCK_A
    col = col % BLOCK_B
    wa = quad_weights(v[0:1])
    wb = quad_weights(v[1:2])
    aw = banded(lax.broadcasted_iota(jnp.int32, (8, LANES), 0) - 1 - row, wa)
    bw = banded(lax.broadcasted_iota(jnp.int32, (BLOCK_B, LANES), 0) - col, wb)
    left = jnp.where(col == 0, wb[0], 0.0)
    right = jnp.where(col == BLOCK_B - 1, wb[2], 0.0)
    scale = jnp.where(live, step_length, 0.0)
    moved = []
    for c in range(2):
        y = None
        for i in range(reach):
            term = aw[i:i + 1] * nodes(slice((c * reach + i) * BLOCK_B, (c * reach + i + 1) * BLOCK_B))
            y = term if y is None else y + term
        y = y * bw
        low = 2 * reach * BLOCK_B + c * 16
        z = aw * (left * nodes(slice(low, low + 8)) + right * nodes(slice(low + 8, low + 16)))
        for k in range(BLOCK_B // 8):
            z = z + y[8 * k:8 * k + 8]
        moved.append(jnp.sum(z, axis=0, keepdims=True) * scale)
    line = lax.broadcasted_iota(jnp.int32, v.shape, 0)
    return v + jnp.where(line == 2, moved[0], jnp.where(line == 3, moved[1], 0.0))


def advance_block(block, source, at, tile_width, nodes_ref, out_ref, cell_ref):
    for j in range(2):
        lanes = slice(at + j * LANES, at + (j + 1) * LANES)
        v = block[8 * j:8 * j + 8, :]
        cell = block[16 + j:17 + j, :]
        out_ref[:, pl.ds(pl.multiple_of(source * 2 * LANES + j * LANES, LANES), LANES)] = weigh(
            v, cell, tile_width, lambda rows, lanes=lanes: nodes_ref[rows, lanes], None)
    cell_ref[pl.ds(source * 2, 2), :] = block[16:18, :].astype(jnp.int32)


def sort_kernel(width, chunk, tile_width, part_ref, key_ref, a_ref, b_ref, blocks_ref,
                hot_ref, base_ref, pick_ref, low_ref, acc_ref, sorted_ref, cells_ref, first_ref, first_smem, local_sem):
    first_ref[...] = jnp.zeros_like(first_ref)
    sort_particles(blocks_ref.shape[0], width, chunk, part_ref, key_ref, a_ref, b_ref, hot_ref, base_ref, pick_ref,
                   low_ref, acc_ref, sorted_ref, cells_ref, first_ref)
    to_smem = pltpu.make_async_copy(first_ref, first_smem, local_sem)
    to_smem.start()
    tops = key_ref.shape[1] // width
    tail = tops * width
    sorted_ref[:, tail:] = jnp.zeros((8, sorted_ref.shape[1] - tail), jnp.float32)
    cells_ref[:, tail:] = jnp.zeros((8, cells_ref.shape[1] - tail), jnp.float32)
    unpack_sorted(tops, width, tile_width, acc_ref, sorted_ref, cells_ref)
    to_smem.wait()

    def cut(owner, carry):
        cut_block(first_smem[0, owner], first_smem[1, owner], sorted_ref, cells_ref, blocks_ref.at[owner])
        return carry

    lax.fori_loop(0, blocks_ref.shape[0], cut, 0, unroll=4)


def exchange_kernel(sizes, blocks_ref, vel_ref, out_ref, cell_ref, held, edge_ref, halo_ref, table_ref,
                    nodes_even, nodes_odd, send_sem, recv_sem, halo_send, halo_recv):
    nx, ny, nz = sizes
    plane = ny * nz
    n = nx * plane
    tile_height, tile_width = vel_ref.shape[1:]
    gx, gy, gz = lax.axis_index("gx"), lax.axis_index("gy"), lax.axis_index("gz")
    column = gy * nz + gz

    def at(dx, dyz, sign):
        x = lax.rem(gx + sign * dx + nx, nx)
        y = lax.rem(gy + sign * (dyz // nz) + ny, ny)
        z = lax.rem(gz + sign * lax.rem(dyz, nz) + nz, nz)
        return x, y, z

    def linear(place):
        return (place[0] * ny + place[1]) * nz + place[2]

    def halo_copy(k, slot):
        da, db = DIRS[k]
        there = column + db
        return pltpu.make_async_remote_copy(
            src_ref=edge_ref, dst_ref=halo_ref.at[slot], send_sem=halo_send.at[k],
            recv_sem=halo_recv.at[slot], device_id=(gx + da, there // nz, lax.rem(there, nz)),
            device_id_type=pl.DeviceIdType.MESH)

    def exists(k):
        da, db = DIRS[k]
        a, b = gx + da, column + db
        return (a >= 0) & (a < nx) & (b >= 0) & (b < plane)

    def hop(q):
        return lax.rem(q, nx), q // nx

    def block_copy(q):
        there = at(*hop(q), 1)
        return pltpu.make_async_remote_copy(
            src_ref=blocks_ref.at[linear(there)], dst_ref=held.at[q],
            send_sem=send_sem.at[q], recv_sem=recv_sem.at[q], device_id=there,
            device_id_type=pl.DeviceIdType.MESH)

    pack_edges(vel_ref, edge_ref)
    for k in range(8):
        @pl.when(exists(k))
        def _(k=k):
            halo_copy(k, 7 - k).start()

        @pl.when(jnp.logical_not(exists(k)))
        def _(k=k):
            halo_ref[k] = jnp.zeros(halo_ref.shape[1:], jnp.float32)

    def dispatch(q, carry):
        block_copy(q).start()
        return carry

    lax.fori_loop(1, n, dispatch, 0)
    held[0] = blocks_ref[linear((gx, gy, gz))]

    for k in range(8):
        @pl.when(exists(k))
        def _(k=k):
            halo_copy(k, k).wait_recv()

    build_table(vel_ref, halo_ref, table_ref, tile_height, tile_width)

    def gather(t, nodes_ref):
        gather_nodes([held.at[2 * t], held.at[2 * t + 1]], tile_width, table_ref, nodes_ref)

    def weigh_pair(t, nodes_ref):
        for i in range(2):
            source = linear(at(*hop(2 * t + i), -1))
            advance_block(held.at[2 * t + i], source, i * 2 * LANES, tile_width, nodes_ref, out_ref, cell_ref)

    block_copy(1).wait_recv()
    gather(0, nodes_even)

    def both(t, carry):
        block_copy(4 * t + 2).wait_recv()
        block_copy(4 * t + 3).wait_recv()
        gather(2 * t + 1, nodes_odd)
        weigh_pair(2 * t, nodes_even)

        @pl.when(t + 1 < n // 4)
        def _():
            block_copy(4 * t + 4).wait_recv()
            block_copy(4 * t + 5).wait_recv()

        gather(jnp.minimum(2 * t + 2, n // 2 - 1), nodes_even)
        weigh_pair(2 * t + 1, nodes_odd)
        return carry

    lax.fori_loop(0, n // 4, both, 0)

    def sent(q, carry):
        block_copy(q).wait_send()
        return carry

    lax.fori_loop(1, n, sent, 0)
    for k in range(8):
        @pl.when(exists(k))
        def _(k=k):
            halo_copy(k, 7 - k).wait_send()


def shards(particles, dest_key, cell_a, cell_b, velocity):
    owners = lax.axis_size(("gx", "gy", "gz"))
    count = particles.shape[1]
    cap = 4 * count // owners
    tile_height, tile_width = velocity.shape[1:]
    assert owners == LANES and cap == 2 * LANES and (tile_height, tile_width) == (256, 128)
    width, chunk = 256, 1024
    tops = count // width
    sizes = tuple(lax.axis_size(name) for name in ("gx", "gy", "gz"))
    in_vmem = pl.BlockSpec(memory_space=pltpu.VMEM)
    blocks = pl.pallas_call(
        functools.partial(sort_kernel, width, chunk, tile_width),
        out_shape=jax.ShapeDtypeStruct((owners, 18, LANES), jnp.float32),
        in_specs=[in_vmem] * 4,
        out_specs=in_vmem,
        scratch_shapes=[
            pltpu.VMEM((owners, count), jnp.bfloat16),
            pltpu.VMEM((tops, owners, LANES), jnp.float32),
            pltpu.VMEM((tops * 18, chunk), jnp.bfloat16),
            pltpu.VMEM((width, chunk), jnp.bfloat16),
            pltpu.VMEM((tops * 18, width), jnp.float32),
            pltpu.VMEM((8, count + 3 * LANES), jnp.float32),
            pltpu.VMEM((8, count + 3 * LANES), jnp.float32),
            pltpu.VMEM((8, LANES), jnp.int32),
            pltpu.SMEM((8, LANES), jnp.int32),
            pltpu.SemaphoreType.DMA,
        ],
    )(particles, dest_key.reshape(1, -1), cell_a.reshape(1, -1), cell_b.reshape(1, -1))
    rows = 12 * BLOCK_B + 32
    binned, binned_cell = pl.pallas_call(
        functools.partial(exchange_kernel, sizes),
        out_shape=(jax.ShapeDtypeStruct((8, owners * cap), jnp.float32),
                   jax.ShapeDtypeStruct((owners * 2, LANES), jnp.int32)),
        in_specs=[in_vmem] * 2,
        out_specs=(in_vmem,) * 2,
        scratch_shapes=[
            pltpu.VMEM((owners, 18, LANES), jnp.float32),
            pltpu.VMEM((8, max(tile_height, tile_width)), jnp.float32),
            pltpu.VMEM((8, 8, max(tile_height, tile_width)), jnp.float32),
            pltpu.VMEM((rows, 2 * 256), jnp.bfloat16),
            pltpu.VMEM((rows, 4 * LANES), jnp.float32),
            pltpu.VMEM((rows, 4 * LANES), jnp.float32),
            pltpu.SemaphoreType.DMA((owners,)),
            pltpu.SemaphoreType.DMA((owners,)),
            pltpu.SemaphoreType.DMA((8,)),
            pltpu.SemaphoreType.DMA((8,)),
        ],
        compiler_params=pltpu.CompilerParams(has_side_effects=True),
    )(blocks, velocity)
    return (binned, binned_cell.reshape(-1))


def solution(mesh):
    in_specs = (
        P(None, ("gx", "gy", "gz")),
        P(("gx", "gy", "gz")),
        P(("gx", "gy", "gz")),
        P(("gx", "gy", "gz")),
        P(None, "gx", ("gy", "gz")),
    )
    out_specs = (P(None, ("gx", "gy", "gz")), P(("gx", "gy", "gz")))
    return jax.shard_map(shards, mesh=mesh, in_specs=in_specs, out_specs=out_specs, check_vma=False)
```

time: 96.5 us -> 84.1 us (0.87)
  the two profiles are of different devices: /device:TPU:1 before, /device:TPU:31 now
where the time goes in v1:
time: 84.1 us; the launch traced here: 83.9 us
  Pallas kernels  80.3 us (95%)
  local copies, waits for them, and re-layouts  2.97 us (4%)
    pallas_call x1, Pallas kernels, shards(): pl.pallas_call(functools.partial(exchange_kernel, sizes), out_shape=(jax....  65.6 us
    pallas_call x1, Pallas kernels, shards(): pl.pallas_call(functools.partial(sort_kernel, width, chunk, tile_width),...  14.7 us
    unnamed x4, local copies, waits for them, and re-layouts  2.97 us

profile of v1, /device:TPU:31, one launch (start us, length us, event | category | flops | bytes accessed | tf_op | source)
XLA Modules:
  0.0 83.9 jit_solution(12273598217103351259)
XLA Ops:
  0.6 14.7 %shard_map.68.blocks_ref = f32[128,18,128]{2,1,0:T(8,128)} custom-call(f32[8,8192]{1,0:T(8,128)} %part_ref.1, s32[1,8192]{1,0:T(1,128)} %bitcast.5, s32[1,8192]{1,0:T(1,128)} %bitcast.6, s32[1,8192]{1,0:T(1,128)} %bitcast.7), custom_call_target="tpu_custom_call" | custom-call | tf_op jit(solution)/shard_map/pallas_call | solution.py:396
  15.4 65.6 %shard_map.69 = (f32[8,32768]{1,0:T(8,128)}, s32[256,128]{1,0:T(8,128)}) custom-call(f32[128,18,128]{2,1,0:T(8,128)} %shard_map.68.blocks_ref, f32[2,256,128]{2,1,0:T(8,128)} %vel_ref.1), custom_call_target="tpu_custom_call" | custom-call | tf_op jit(solution)/shard_map/pallas_call | solution.py:415
  81.0 0.0 copy-start
  81.0 2.3 %copy.9 = f32[8,32768]{1,0:T(8,128)} copy(f32[8,32768]{1,0:T(8,128)} %get-tuple-element.8) | data formatting | bytes 2097152
  83.3 0.0 copy-done
  83.3 0.7 copy.10
Async XLA Ops:
  81.0 2.3 %copy-start = (s32[256,128]{1,0:T(8,128)S(1)}, s32[256,128]{1,0:T(8,128)}, u32[]{:S(2)}) copy-start(s32[256,128]{1,0:T(8,128)} %get-tuple-element.5) | copy-start | bytes 393220

commit v2 on v1

--- a/solution.py
+++ b/solution.py
@@ -47,33 +47,34 @@
     count = key_ref.shape[1]
     owner_rows = narrow_iota((owners, width), 0)
     ones = jnp.ones((width, LANES), jnp.bfloat16)
-    base_ref[...] = jnp.zeros_like(base_ref)
+    owner_ids = lax.broadcasted_iota(jnp.int32, (owners, LANES), 0)
     tops = count // width
 
-    def count_chunk(index, seen):
+    def count_chunk(index, carry):
+        seen, tally = carry
         for part in range(chunk // width):
             start = pl.multiple_of(index * chunk + part * width, width)
-            keys = key_ref[:, pl.ds(start, width)].astype(jnp.float32).astype(jnp.bfloat16)
-            hot = one_hot(owner_rows, keys)
+            keys = key_ref[:, pl.ds(start, width)]
+            hot = one_hot(owner_rows, keys.astype(jnp.float32).astype(jnp.bfloat16))
             hot_ref[:, pl.ds(start, width)] = hot
             base_ref[index * (chunk // width) + part] = seen
             seen = seen + jnp.dot(hot, ones, preferred_element_type=jnp.float32)
-        return seen
-
-    total = lax.fori_loop(0, count // chunk, count_chunk, jnp.zeros((owners, LANES), jnp.float32))
+            for j in range(width // LANES):
+                tally = tally + jnp.where(owner_ids == keys[:, j * LANES:(j + 1) * LANES], 1, 0)
+        return seen, tally
+
+    total, tally = lax.fori_loop(0, count // chunk, count_chunk, (
+        jnp.zeros((owners, LANES), jnp.float32), jnp.zeros((owners, LANES), jnp.int32)))
+    tally = jnp.sum(tally, axis=1, keepdims=True)
     below = (lax.broadcasted_iota(jnp.int32, (owners, owners), 1)
              < lax.broadcasted_iota(jnp.int32, (owners, owners), 0)).astype(jnp.float32).astype(jnp.bfloat16)
     first = jnp.dot(below, total.astype(jnp.bfloat16), preferred_element_type=jnp.float32)
-    eye = (lax.broadcasted_iota(jnp.int32, (owners, LANES), 1)
-           == lax.broadcasted_iota(jnp.int32, (owners, LANES), 0))
-    firsts = jnp.sum(jnp.where(eye, first, 0.0), axis=0, keepdims=True)
-    totals = jnp.sum(jnp.where(eye, total, 0.0), axis=0, keepdims=True)
-    table_ref[0:1, :] = firsts.astype(jnp.int32)
-    table_ref[1:2, :] = totals.astype(jnp.int32)
+    lane_ids = lax.broadcasted_iota(jnp.int32, (owners, LANES), 1)
+    table_ref[0:1, :] = jnp.sum(jnp.where(owner_ids < lane_ids, tally, 0), axis=0, keepdims=True)
+    table_ref[1:2, :] = jnp.sum(jnp.where(owner_ids == lane_ids, tally, 0), axis=0, keepdims=True)
 
     upper = (lax.broadcasted_iota(jnp.int32, (width, width), 0)
              < lax.broadcasted_iota(jnp.int32, (width, width), 1)).astype(jnp.float32).astype(jnp.bfloat16)
-    owner_ids = lax.broadcasted_iota(jnp.int32, (owners, LANES), 0)
     low_rows = narrow_iota((width, width), 0)
     top_rows = narrow_iota((tops, width), 0)
     zero = jnp.zeros((), jnp.bfloat16)
@@ -115,26 +116,29 @@
 
 def unpack_sorted(tops, width, tile_width, acc_ref, sorted_ref, cells_ref):
     cells = acc_ref[tops * 16:tops * 17, :] * float(tile_width) + acc_ref[tops * 17:tops * 18, :]
+    per = width // LANES
     for i in range(tops):
-        at = slice(i * width, (i + 1) * width)
-        sorted_ref[:, at] = acc_ref[i * 16:i * 16 + 8, :] + acc_ref[i * 16 + 8:i * 16 + 16, :]
-        cells_ref[0:1, at] = cells[i:i + 1, :]
+        rows = acc_ref[i * 16:i * 16 + 8, :] + acc_ref[i * 16 + 8:i * 16 + 16, :]
+        for j in range(per):
+            at = slice(j * LANES, (j + 1) * LANES)
+            sorted_ref[i * per + j] = rows[:, at]
+            cells_ref[i * per + j, 0:1] = cells[i:i + 1, at]
 
 
 def cut_block(first, size, sorted_ref, cells_ref, out):
-    base = pl.multiple_of((first // LANES) * LANES, LANES)
-    shift = first - base
-    back = lax.rem(LANES - shift, LANES)
+    base = first // LANES
+    shift = first - base * LANES
+    back = LANES - shift
     lane = lax.broadcasted_iota(jnp.int32, (8, LANES), 1)
-    near = lane < LANES - shift
-    for source, rows in ((sorted_ref, 8), (cells_ref, 1)):
-        turned = [pltpu.roll(source[:, pl.ds(base + j * LANES, LANES)], back, 1) for j in range(3)]
-        for j in range(2):
-            piece = jnp.where(near, turned[j], turned[j + 1])
-            if rows == 8:
-                out[8 * j:8 * j + 8, :] = jnp.where(lane + j * LANES < size, piece, 0.0)
-            else:
-                out[16 + j:17 + j, :] = jnp.where(lane + j * LANES < size, piece, -1.0)[0:1]
+    near = lane < back
+    turned = [pltpu.roll(sorted_ref[base + j], back, 1) for j in range(3)]
+    for j in range(2):
+        piece = jnp.where(near, turned[j], turned[j + 1])
+        out[8 * j:8 * j + 8, :] = jnp.where(lane + j * LANES < size, piece, 0.0)
+    turned = [pltpu.roll(cells_ref[base + j], back, 1) for j in range(3)]
+    for j in range(2):
+        piece = jnp.where(near, turned[j], turned[j + 1])
+        out[16 + j:17 + j, :] = jnp.where(lane + j * LANES < size, piece, -1.0)[0:1]
 
 
 def build_table(vel_ref, halo_ref, table_ref, tile_height, tile_width):
@@ -258,29 +262,10 @@
     cell_ref[pl.ds(source * 2, 2), :] = block[16:18, :].astype(jnp.int32)
 
 
-def sort_kernel(width, chunk, tile_width, part_ref, key_ref, a_ref, b_ref, blocks_ref,
-                hot_ref, base_ref, pick_ref, low_ref, acc_ref, sorted_ref, cells_ref, first_ref, first_smem, local_sem):
-    first_ref[...] = jnp.zeros_like(first_ref)
-    sort_particles(blocks_ref.shape[0], width, chunk, part_ref, key_ref, a_ref, b_ref, hot_ref, base_ref, pick_ref,
-                   low_ref, acc_ref, sorted_ref, cells_ref, first_ref)
-    to_smem = pltpu.make_async_copy(first_ref, first_smem, local_sem)
-    to_smem.start()
-    tops = key_ref.shape[1] // width
-    tail = tops * width
-    sorted_ref[:, tail:] = jnp.zeros((8, sorted_ref.shape[1] - tail), jnp.float32)
-    cells_ref[:, tail:] = jnp.zeros((8, cells_ref.shape[1] - tail), jnp.float32)
-    unpack_sorted(tops, width, tile_width, acc_ref, sorted_ref, cells_ref)
-    to_smem.wait()
-
-    def cut(owner, carry):
-        cut_block(first_smem[0, owner], first_smem[1, owner], sorted_ref, cells_ref, blocks_ref.at[owner])
-        return carry
-
-    lax.fori_loop(0, blocks_ref.shape[0], cut, 0, unroll=4)
-
-
-def exchange_kernel(sizes, blocks_ref, vel_ref, out_ref, cell_ref, held, edge_ref, halo_ref, table_ref,
-                    nodes_even, nodes_odd, send_sem, recv_sem, halo_send, halo_recv):
+def exchange_kernel(sizes, width, chunk, part_ref, key_ref, a_ref, b_ref, vel_ref, out_ref, cell_ref,
+                    hot_ref, base_ref, pick_ref, low_ref, acc_ref, sorted_ref, cells_ref, first_ref, first_smem,
+                    outgoing, held, edge_ref, halo_ref, table_ref, nodes_even, nodes_odd,
+                    send_sem, recv_sem, halo_send, halo_recv, local_sem):
     nx, ny, nz = sizes
     plane = ny * nz
     n = nx * plane
@@ -316,11 +301,30 @@
     def block_copy(q):
         there = at(*hop(q), 1)
         return pltpu.make_async_remote_copy(
-            src_ref=blocks_ref.at[linear(there)], dst_ref=held.at[q],
+            src_ref=outgoing.at[q], dst_ref=held.at[q],
             send_sem=send_sem.at[q], recv_sem=recv_sem.at[q], device_id=there,
             device_id_type=pl.DeviceIdType.MESH)
 
+    barrier = pltpu.get_barrier_semaphore()
+
+    def greet(q, carry):
+        pl.semaphore_signal(barrier, inc=1, device_id=at(*hop(q), 1), device_id_type=pl.DeviceIdType.MESH)
+        return carry
+
+    lax.fori_loop(1, n, greet, 0)
     pack_edges(vel_ref, edge_ref)
+    first_ref[...] = jnp.zeros_like(first_ref)
+    sort_particles(n, width, chunk, part_ref, key_ref, a_ref, b_ref, hot_ref, base_ref, pick_ref,
+                   low_ref, acc_ref, sorted_ref, cells_ref, first_ref)
+    to_smem = pltpu.make_async_copy(first_ref, first_smem, local_sem)
+    to_smem.start()
+    tops = key_ref.shape[1] // width
+    tail = tops * width // LANES
+    sorted_ref[tail:] = jnp.zeros((3, 8, LANES), jnp.float32)
+    cells_ref[tail:] = jnp.zeros((3, 8, LANES), jnp.float32)
+    unpack_sorted(tops, width, tile_width, acc_ref, sorted_ref, cells_ref)
+    to_smem.wait()
+    pl.semaphore_wait(barrier, n - 1)
     for k in range(8):
         @pl.when(exists(k))
         def _(k=k):
@@ -330,12 +334,17 @@
         def _(k=k):
             halo_ref[k] = jnp.zeros(halo_ref.shape[1:], jnp.float32)
 
+    def cut(q, out):
+        owner = linear(at(*hop(q), 1))
+        cut_block(first_smem[0, owner], first_smem[1, owner], sorted_ref, cells_ref, out)
+
     def dispatch(q, carry):
+        cut(q, outgoing.at[q])
         block_copy(q).start()
         return carry
 
     lax.fori_loop(1, n, dispatch, 0)
-    held[0] = blocks_ref[linear((gx, gy, gz))]
+    cut(0, held.at[0])
 
     for k in range(8):
         @pl.when(exists(k))
@@ -393,32 +402,24 @@
     tops = count // width
     sizes = tuple(lax.axis_size(name) for name in ("gx", "gy", "gz"))
     in_vmem = pl.BlockSpec(memory_space=pltpu.VMEM)
-    blocks = pl.pallas_call(
-        functools.partial(sort_kernel, width, chunk, tile_width),
-        out_shape=jax.ShapeDtypeStruct((owners, 18, LANES), jnp.float32),
-        in_specs=[in_vmem] * 4,
-        out_specs=in_vmem,
+    rows = 12 * BLOCK_B + 32
+    binned, binned_cell = pl.pallas_call(
+        functools.partial(exchange_kernel, sizes, width, chunk),
+        out_shape=(jax.ShapeDtypeStruct((8, owners * cap), jnp.float32),
+                   jax.ShapeDtypeStruct((owners * 2, LANES), jnp.int32)),
+        in_specs=[in_vmem] * 5,
+        out_specs=(in_vmem,) * 2,
         scratch_shapes=[
             pltpu.VMEM((owners, count), jnp.bfloat16),
             pltpu.VMEM((tops, owners, LANES), jnp.float32),
             pltpu.VMEM((tops * 18, chunk), jnp.bfloat16),
             pltpu.VMEM((width, chunk), jnp.bfloat16),
             pltpu.VMEM((tops * 18, width), jnp.float32),
-            pltpu.VMEM((8, count + 3 * LANES), jnp.float32),
-            pltpu.VMEM((8, count + 3 * LANES), jnp.float32),
+            pltpu.VMEM((count // LANES + 3, 8, LANES), jnp.float32),
+            pltpu.VMEM((count // LANES + 3, 8, LANES), jnp.float32),
             pltpu.VMEM((8, LANES), jnp.int32),
             pltpu.SMEM((8, LANES), jnp.int32),
-            pltpu.SemaphoreType.DMA,
-        ],
-    )(particles, dest_key.reshape(1, -1), cell_a.reshape(1, -1), cell_b.reshape(1, -1))
-    rows = 12 * BLOCK_B + 32
-    binned, binned_cell = pl.pallas_call(
-        functools.partial(exchange_kernel, sizes),
-        out_shape=(jax.ShapeDtypeStruct((8, owners * cap), jnp.float32),
-                   jax.ShapeDtypeStruct((owners * 2, LANES), jnp.int32)),
-        in_specs=[in_vmem] * 2,
-        out_specs=(in_vmem,) * 2,
-        scratch_shapes=[
+            pltpu.VMEM((owners, 18, LANES), jnp.float32),
             pltpu.VMEM((owners, 18, LANES), jnp.float32),
             pltpu.VMEM((8, max(tile_height, tile_width)), jnp.float32),
             pltpu.VMEM((8, 8, max(tile_height, tile_width)), jnp.float32),
@@ -429,9 +430,10 @@
             pltpu.SemaphoreType.DMA((owners,)),
             pltpu.SemaphoreType.DMA((8,)),
             pltpu.SemaphoreType.DMA((8,)),
+            pltpu.SemaphoreType.DMA,
         ],
-        compiler_params=pltpu.CompilerParams(has_side_effects=True),
-    )(blocks, velocity)
+        compiler_params=pltpu.CompilerParams(collective_id=0, has_side_effects=True),
+    )(particles, dest_key.reshape(1, -1), cell_a.reshape(1, -1), cell_b.reshape(1, -1), velocity)
     return (binned, binned_cell.reshape(-1))
 
 

time: 84.1 us -> 72 us (0.86)
  the two profiles are of different devices: /device:TPU:31 before, /device:TPU:1 now
where the time goes in v2:
time: 72 us; the launch traced here: 71.9 us
  Pallas kernels  68.2 us (95%)
  local copies, waits for them, and re-layouts  2.97 us (4%)
    pallas_call x1, Pallas kernels, shards(): pl.pallas_call(functools.partial(exchange_kernel, sizes, width, chunk), o...  68.2 us
    unnamed x4, local copies, waits for them, and re-layouts  2.97 us

profile of v2, /device:TPU:1, one launch (start us, length us, event | category | flops | bytes accessed | tf_op | source)
XLA Modules:
  0.0 71.9 jit_solution(4583820242927592338)
XLA Ops:
  0.6 68.2 %shard_map.68 = (f32[8,32768]{1,0:T(8,128)}, s32[256,128]{1,0:T(8,128)}) custom-call(f32[8,8192]{1,0:T(8,128)} %part_ref.1, s32[1,8192]{1,0:T(1,128)} %bitcast.5, s32[1,8192]{1,0:T(1,128)} %bitcast.6, s32[1,8192]{1,0:T(1,128)} %bitcast.7, f32[2,256,128]{2,1,0:T(8,128)} %vel_ref.1), custom_call_target="tpu_custom_call" | custom-call | tf_op jit(solution)/shard_map/pallas_call | solution.py:406
  68.9 0.0 copy-start
  68.9 2.3 %copy.9 = f32[8,32768]{1,0:T(8,128)} copy(f32[8,32768]{1,0:T(8,128)} %get-tuple-element.8) | data formatting | bytes 2097152
  71.2 0.0 copy-done
  71.2 0.7 copy.10
Async XLA Ops:
  68.9 2.3 %copy-start = (s32[256,128]{1,0:T(8,128)S(1)}, s32[256,128]{1,0:T(8,128)}, u32[]{:S(2)}) copy-start(s32[256,128]{1,0:T(8,128)} %get-tuple-element.5) | copy-start | bytes 393220

commit v3 on v2

--- a/solution.py
+++ b/solution.py
@@ -42,7 +42,7 @@
         edge_ref[4 * c + 3:4 * c + 4, :tile_height] = turned[tile_width - 1:]
 
 
-def sort_particles(owners, width, chunk, part_ref, key_ref, a_ref, b_ref,
+def sort_particles(aside, owners, width, chunk, part_ref, key_ref, a_ref, b_ref,
                    hot_ref, base_ref, pick_ref, low_ref, acc_ref, sorted_ref, cells_ref, table_ref):
     count = key_ref.shape[1]
     owner_rows = narrow_iota((owners, width), 0)
@@ -52,6 +52,7 @@
 
     def count_chunk(index, carry):
         seen, tally = carry
+        aside(index)
         for part in range(chunk // width):
             start = pl.multiple_of(index * chunk + part * width, width)
             keys = key_ref[:, pl.ds(start, width)]
@@ -111,7 +112,7 @@
         acc_ref[...] += lax.dot_general(pick_ref[...], low_ref[...], NT, preferred_element_type=jnp.float32)
         return carry
 
-    lax.fori_loop(0, count // chunk, place_chunk, 0)
+    lax.fori_loop(0, count // chunk, place_chunk, 0, unroll=2)
 
 
 def unpack_sorted(tops, width, tile_width, acc_ref, sorted_ref, cells_ref):
@@ -296,7 +297,11 @@
         return (a >= 0) & (a < nx) & (b >= 0) & (b < plane)
 
     def hop(q):
-        return lax.rem(q, nx), q // nx
+        core, r = lax.rem(q, nz), q // nz
+        z = lax.rem(r, nx)
+        x = lax.rem(r + r // nx, 4)
+        y = lax.rem(r + r // (4 * nx), ny // 4)
+        return z, (y * 4 + x) * nz + core
 
     def block_copy(q):
         there = at(*hop(q), 1)
@@ -311,10 +316,16 @@
         pl.semaphore_signal(barrier, inc=1, device_id=at(*hop(q), 1), device_id_type=pl.DeviceIdType.MESH)
         return carry
 
-    lax.fori_loop(1, n, greet, 0)
+    share = (n - 1) // 8
+    lax.fori_loop(8 * share + 1, n, greet, 0)
+
+    def greet_some(index):
+        for i in range(share):
+            greet(index * share + i + 1, 0)
+
     pack_edges(vel_ref, edge_ref)
     first_ref[...] = jnp.zeros_like(first_ref)
-    sort_particles(n, width, chunk, part_ref, key_ref, a_ref, b_ref, hot_ref, base_ref, pick_ref,
+    sort_particles(greet_some, n, width, chunk, part_ref, key_ref, a_ref, b_ref, hot_ref, base_ref, pick_ref,
                    low_ref, acc_ref, sorted_ref, cells_ref, first_ref)
     to_smem = pltpu.make_async_copy(first_ref, first_smem, local_sem)
     to_smem.start()
@@ -334,17 +345,22 @@
         def _(k=k):
             halo_ref[k] = jnp.zeros(halo_ref.shape[1:], jnp.float32)
 
-    def cut(q, out):
-        owner = linear(at(*hop(q), 1))
-        cut_block(first_smem[0, owner], first_smem[1, owner], sorted_ref, cells_ref, out)
-
-    def dispatch(q, carry):
-        cut(q, outgoing.at[q])
-        block_copy(q).start()
-        return carry
-
-    lax.fori_loop(1, n, dispatch, 0)
-    cut(0, held.at[0])
+    def dispatch(p, carry):
+        for i in range(8):
+            q = p * 8 + i
+            owner = linear(at(*hop(q), 1))
+            cut_block(first_smem[0, owner], first_smem[1, owner], sorted_ref, cells_ref, outgoing.at[q])
+
+        @pl.when(p > 0)
+        def _():
+            block_copy(p * 8).start()
+
+        for i in range(1, 8):
+            block_copy(p * 8 + i).start()
+        return carry
+
+    lax.fori_loop(0, n // 8, dispatch, 0)
+    held[0] = outgoing[0]
 
     for k in range(8):
         @pl.when(exists(k))
@@ -361,25 +377,26 @@
             source = linear(at(*hop(2 * t + i), -1))
             advance_block(held.at[2 * t + i], source, i * 2 * LANES, tile_width, nodes_ref, out_ref, cell_ref)
 
+    group = 16
     block_copy(1).wait_recv()
     gather(0, nodes_even)
 
-    def both(t, carry):
-        block_copy(4 * t + 2).wait_recv()
-        block_copy(4 * t + 3).wait_recv()
-        gather(2 * t + 1, nodes_odd)
-        weigh_pair(2 * t, nodes_even)
-
-        @pl.when(t + 1 < n // 4)
-        def _():
-            block_copy(4 * t + 4).wait_recv()
-            block_copy(4 * t + 5).wait_recv()
-
-        gather(jnp.minimum(2 * t + 2, n // 2 - 1), nodes_even)
-        weigh_pair(2 * t + 1, nodes_odd)
-        return carry
-
-    lax.fori_loop(0, n // 4, both, 0)
+    def arrive(q, carry):
+        block_copy(q).wait_recv()
+        return carry
+
+    def one_group(p, carry):
+        lax.fori_loop(p * group + 2, jnp.minimum((p + 1) * group + 2, n), arrive, 0)
+        first = p * (group // 2)
+
+        for t in range(group // 4):
+            gather(first + 2 * t + 1, nodes_odd)
+            weigh_pair(first + 2 * t, nodes_even)
+            gather(jnp.minimum(first + 2 * t + 2, n // 2 - 1), nodes_even)
+            weigh_pair(first + 2 * t + 1, nodes_odd)
+        return carry
+
+    lax.fori_loop(0, n // group, one_group, 0)
 
     def sent(q, carry):
         block_copy(q).wait_send()

time: 72 us -> 58.6 us (0.81); the launches traced: 71.9 us -> 57.5 us
  Pallas kernels: 68.2 us -> 53.9 us
    pallas_call x1, Pallas kernels: 68.2 us -> 53.9 us  [shards(): pl.pallas_call(functools.partial(exchange_kernel, sizes, width, chunk), o...]
where the time goes in v3:
time: 58.6 us; the launch traced here: 57.5 us
  Pallas kernels  53.9 us (92%)
  local copies, waits for them, and re-layouts  2.97 us (5%)
  between operations  0.65 us (1%)
    pallas_call x1, Pallas kernels, shards(): pl.pallas_call(functools.partial(exchange_kernel, sizes, width, chunk), o...  53.9 us
    unnamed x4, local copies, waits for them, and re-layouts  2.97 us

profile of v3, /device:TPU:1, one launch (start us, length us, event | category | flops | bytes accessed | tf_op | source)
XLA Modules:
  0.0 57.5 jit_solution(5629784133759195632)
XLA Ops:
  0.6 53.9 %shard_map.68 = (f32[8,32768]{1,0:T(8,128)}, s32[256,128]{1,0:T(8,128)}) custom-call(f32[8,8192]{1,0:T(8,128)} %part_ref.1, s32[1,8192]{1,0:T(1,128)} %bitcast.5, s32[1,8192]{1,0:T(1,128)} %bitcast.6, s32[1,8192]{1,0:T(1,128)} %bitcast.7, f32[2,256,128]{2,1,0:T(8,128)} %vel_ref.1), custom_call_target="tpu_custom_call" | custom-call | tf_op jit(solution)/shard_map/pallas_call | solution.py:423
  54.5 0.0 copy-start
  54.5 2.3 %copy.9 = f32[8,32768]{1,0:T(8,128)} copy(f32[8,32768]{1,0:T(8,128)} %get-tuple-element.8) | data formatting | bytes 2097152
  56.8 0.0 copy-done
  56.8 0.7 %copy.10 = s32[32768]{0:T(1024)} copy(s32[32768]{0:T(1024)S(1)} %bitcast.4) | data formatting | bytes 262144
Async XLA Ops:
  54.5 2.3 %copy-start = (s32[256,128]{1,0:T(8,128)S(1)}, s32[256,128]{1,0:T(8,128)}, u32[]{:S(2)}) copy-start(s32[256,128]{1,0:T(8,128)} %get-tuple-element.5) | copy-start | bytes 393220

commit v4 on v3

--- a/solution.py
+++ b/solution.py
@@ -52,7 +52,6 @@
 
     def count_chunk(index, carry):
         seen, tally = carry
-        aside(index)
         for part in range(chunk // width):
             start = pl.multiple_of(index * chunk + part * width, width)
             keys = key_ref[:, pl.ds(start, width)]
@@ -112,7 +111,10 @@
         acc_ref[...] += lax.dot_general(pick_ref[...], low_ref[...], NT, preferred_element_type=jnp.float32)
         return carry
 
-    lax.fori_loop(0, count // chunk, place_chunk, 0, unroll=2)
+    half = count // chunk // 2
+    lax.fori_loop(0, half, place_chunk, 0, unroll=2)
+    aside()
+    lax.fori_loop(half, 2 * half, place_chunk, 0, unroll=2)
 
 
 def unpack_sorted(tops, width, tile_width, acc_ref, sorted_ref, cells_ref):
@@ -266,18 +268,21 @@
 def exchange_kernel(sizes, width, chunk, part_ref, key_ref, a_ref, b_ref, vel_ref, out_ref, cell_ref,
                     hot_ref, base_ref, pick_ref, low_ref, acc_ref, sorted_ref, cells_ref, first_ref, first_smem,
                     outgoing, held, edge_ref, halo_ref, table_ref, nodes_even, nodes_odd,
-                    send_sem, recv_sem, halo_send, halo_recv, local_sem):
+                    send_sem, recv_sem, halo_send, halo_recv, local_sem, row_sem):
     nx, ny, nz = sizes
     plane = ny * nz
     n = nx * plane
+    group = 16
     tile_height, tile_width = vel_ref.shape[1:]
     gx, gy, gz = lax.axis_index("gx"), lax.axis_index("gy"), lax.axis_index("gz")
     column = gy * nz + gz
 
+    assert (nx, ny, nz) == (4, 16, 2)
+
     def at(dx, dyz, sign):
-        x = lax.rem(gx + sign * dx + nx, nx)
-        y = lax.rem(gy + sign * (dyz // nz) + ny, ny)
-        z = lax.rem(gz + sign * lax.rem(dyz, nz) + nz, nz)
+        x = (gx + sign * dx) & (nx - 1)
+        y = (gy + sign * (dyz >> 1)) & (ny - 1)
+        z = gz ^ (dyz & 1)
         return x, y, z
 
     def linear(place):
@@ -297,35 +302,46 @@
         return (a >= 0) & (a < nx) & (b >= 0) & (b < plane)
 
     def hop(q):
-        core, r = lax.rem(q, nz), q // nz
-        z = lax.rem(r, nx)
-        x = lax.rem(r + r // nx, 4)
-        y = lax.rem(r + r // (4 * nx), ny // 4)
+        core, r = q & 1, q >> 1
+        z = r & 3
+        x = (r + (r >> 2)) & 3
+        y = (r + (r >> 4)) & 3
         return z, (y * 4 + x) * nz + core
 
     def block_copy(q):
-        there = at(*hop(q), 1)
         return pltpu.make_async_remote_copy(
             src_ref=outgoing.at[q], dst_ref=held.at[q],
-            send_sem=send_sem.at[q], recv_sem=recv_sem.at[q], device_id=there,
+            send_sem=send_sem, recv_sem=recv_sem.at[(q + group - 2) >> 4], device_id=at(*hop(q), 1),
             device_id_type=pl.DeviceIdType.MESH)
 
+    def arrived(first, size, p):
+        some = pl.ds(first, size)
+        return pltpu.make_async_remote_copy(
+            src_ref=outgoing.at[some], dst_ref=held.at[some], send_sem=send_sem, recv_sem=recv_sem.at[p],
+            device_id=at(*hop(1), 1), device_id_type=pl.DeviceIdType.MESH)
+
     barrier = pltpu.get_barrier_semaphore()
 
-    def greet(q, carry):
-        pl.semaphore_signal(barrier, inc=1, device_id=at(*hop(q), 1), device_id_type=pl.DeviceIdType.MESH)
+    def row_peer(i):
+        return (gx + (i >> 1)) & (nx - 1), gy, gz ^ (i & 1)
+
+    def greet(i, carry):
+        pl.semaphore_signal(barrier, inc=1, device_id=(gx, (gy + i) & (ny - 1), gz),
+                            device_id_type=pl.DeviceIdType.MESH)
         return carry
 
-    share = (n - 1) // 8
-    lax.fori_loop(8 * share + 1, n, greet, 0)
-
-    def greet_some(index):
-        for i in range(share):
-            greet(index * share + i + 1, 0)
+    lax.fori_loop(1, ny, greet, 0)
+    for i in range(1, nx * nz):
+        pl.semaphore_signal(barrier, inc=1, device_id=row_peer(i), device_id_type=pl.DeviceIdType.MESH)
+
+    def pass_on():
+        pl.semaphore_wait(barrier, ny - 1 + nx * nz - 1)
+        for i in range(1, nx * nz):
+            pl.semaphore_signal(row_sem, inc=1, device_id=row_peer(i), device_id_type=pl.DeviceIdType.MESH)
 
     pack_edges(vel_ref, edge_ref)
     first_ref[...] = jnp.zeros_like(first_ref)
-    sort_particles(greet_some, n, width, chunk, part_ref, key_ref, a_ref, b_ref, hot_ref, base_ref, pick_ref,
+    sort_particles(pass_on, n, width, chunk, part_ref, key_ref, a_ref, b_ref, hot_ref, base_ref, pick_ref,
                    low_ref, acc_ref, sorted_ref, cells_ref, first_ref)
     to_smem = pltpu.make_async_copy(first_ref, first_smem, local_sem)
     to_smem.start()
@@ -335,7 +351,7 @@
     cells_ref[tail:] = jnp.zeros((3, 8, LANES), jnp.float32)
     unpack_sorted(tops, width, tile_width, acc_ref, sorted_ref, cells_ref)
     to_smem.wait()
-    pl.semaphore_wait(barrier, n - 1)
+    pl.semaphore_wait(row_sem, nx * nz - 1)
     for k in range(8):
         @pl.when(exists(k))
         def _(k=k):
@@ -377,16 +393,18 @@
             source = linear(at(*hop(2 * t + i), -1))
             advance_block(held.at[2 * t + i], source, i * 2 * LANES, tile_width, nodes_ref, out_ref, cell_ref)
 
-    group = 16
-    block_copy(1).wait_recv()
+    arrived(1, 1, 0).wait_recv()
     gather(0, nodes_even)
 
-    def arrive(q, carry):
-        block_copy(q).wait_recv()
-        return carry
-
     def one_group(p, carry):
-        lax.fori_loop(p * group + 2, jnp.minimum((p + 1) * group + 2, n), arrive, 0)
+        @pl.when(p < n // group - 1)
+        def _():
+            arrived(p * group + 2, group, p + 1).wait_recv()
+
+        @pl.when(p == n // group - 1)
+        def _():
+            arrived(n - group + 2, group - 2, n // group).wait_recv()
+
         first = p * (group // 2)
 
         for t in range(group // 4):
@@ -398,11 +416,7 @@
 
     lax.fori_loop(0, n // group, one_group, 0)
 
-    def sent(q, carry):
-        block_copy(q).wait_send()
-        return carry
-
-    lax.fori_loop(1, n, sent, 0)
+    arrived(1, n - 1, 0).wait_send()
     for k in range(8):
         @pl.when(exists(k))
         def _(k=k):
@@ -443,11 +457,12 @@
             pltpu.VMEM((rows, 2 * 256), jnp.bfloat16),
             pltpu.VMEM((rows, 4 * LANES), jnp.float32),
             pltpu.VMEM((rows, 4 * LANES), jnp.float32),
-            pltpu.SemaphoreType.DMA((owners,)),
-            pltpu.SemaphoreType.DMA((owners,)),
+            pltpu.SemaphoreType.DMA,
+            pltpu.SemaphoreType.DMA((owners // 16 + 1,)),
             pltpu.SemaphoreType.DMA((8,)),
             pltpu.SemaphoreType.DMA((8,)),
             pltpu.SemaphoreType.DMA,
+            pltpu.SemaphoreType.REGULAR,
         ],
         compiler_params=pltpu.CompilerParams(collective_id=0, has_side_effects=True),
     )(particles, dest_key.reshape(1, -1), cell_a.reshape(1, -1), cell_b.reshape(1, -1), velocity)

time: 58.6 us -> 49.9 us (0.85)
  the two profiles are of different devices: /device:TPU:1 before, /device:TPU:95 now
where the time goes in v4:
time: 49.9 us; the launch traced here: 49.8 us
  Pallas kernels  46.2 us (93%)
  local copies, waits for them, and re-layouts  2.97 us (6%)
  between operations  0.65 us (1%)
    pallas_call x1, Pallas kernels, shards(): pl.pallas_call(functools.partial(exchange_kernel, sizes, width, chunk), o...  46.2 us
    unnamed x4, local copies, waits for them, and re-layouts  2.97 us

profile of v4, /device:TPU:95, one launch (start us, length us, event | category | flops | bytes accessed | tf_op | source)
XLA Modules:
  0.0 49.8 jit_solution(6451639415538541647)
XLA Ops:
  0.6 46.2 %shard_map.68 = (f32[8,32768]{1,0:T(8,128)}, s32[256,128]{1,0:T(8,128)}) custom-call(f32[8,8192]{1,0:T(8,128)} %part_ref.1, s32[1,8192]{1,0:T(1,128)} %bitcast.5, s32[1,8192]{1,0:T(1,128)} %bitcast.6, s32[1,8192]{1,0:T(1,128)} %bitcast.7, f32[2,256,128]{2,1,0:T(8,128)} %vel_ref.1), custom_call_target="tpu_custom_call" | custom-call | tf_op jit(solution)/shard_map/pallas_call | solution.py:437
  46.8 0.0 copy-start
  46.8 2.3 %copy.9 = f32[8,32768]{1,0:T(8,128)} copy(f32[8,32768]{1,0:T(8,128)} %get-tuple-element.8) | data formatting | bytes 2097152
  49.1 0.0 copy-done
  49.1 0.7 %copy.10 = s32[32768]{0:T(1024)} copy(s32[32768]{0:T(1024)S(1)} %bitcast.4) | data formatting | bytes 262144
Async XLA Ops:
  46.8 2.3 %copy-start = (s32[256,128]{1,0:T(8,128)S(1)}, s32[256,128]{1,0:T(8,128)}, u32[]{:S(2)}) copy-start(s32[256,128]{1,0:T(8,128)} %get-tuple-element.5) | copy-start | bytes 393220

commit v5 on v4

--- a/solution.py
+++ b/solution.py
@@ -10,6 +10,8 @@
 step_length = 0.5
 NT = (((1,), (1,)), ((), ()))
 LANES = 128
+NARROW = jnp.float8_e4m3fn
+TERMS, TOP = 3, 256.0
 BLOCK_A, BLOCK_B = 4, 32
 DIRS = ((-1, -1), (-1, 0), (-1, 1), (0, -1), (0, 1), (1, -1), (1, 0), (1, 1))
 
@@ -159,6 +161,15 @@
     def beside(da, db, row):
         return halo_ref[DIRS.index((da, db)), row:row + 1, :]
 
+    largest = jnp.maximum(jnp.max(jnp.abs(vel_ref[0]), axis=0, keepdims=True),
+                          jnp.max(jnp.abs(vel_ref[1]), axis=0, keepdims=True))
+    border = jnp.max(jnp.abs(halo_ref[0]), axis=0, keepdims=True)
+    for k in range(1, 8):
+        border = jnp.maximum(border, jnp.max(jnp.abs(halo_ref[k]), axis=0, keepdims=True))
+    largest = jnp.maximum(largest, jnp.maximum(border[:, :LANES], border[:, LANES:]))
+    largest = jnp.maximum(jnp.max(largest, axis=1, keepdims=True), 1e-30)
+    scale = TOP / largest
+    extras = [[[] for _ in range(2)] for _ in range(TERMS)]
     for c in range(2):
         own = jnp.transpose(vel_ref[c])
         left = beside(0, -1, 4 * c + 3)[:, :tile_height]
@@ -176,11 +187,14 @@
         ends = jnp.concatenate([outer(-1, 4 * c + 1), outer(1, 4 * c),
                                 jnp.zeros((LANES - 2, 2 * LANES), jnp.float32)], axis=0)
         full = jnp.concatenate([body, jnp.transpose(ends)[:width]], axis=1)
-        high = rounded(full)
-        both = jnp.concatenate([high, full - high], axis=0).astype(jnp.bfloat16)
-        spread = jnp.dot(both, select, preferred_element_type=jnp.float32)
+        rest, terms = full * scale, []
+        for _ in range(TERMS):
+            terms.append(rest.astype(NARROW).astype(jnp.float32))
+            rest = rest - terms[-1]
+        spread = jnp.dot(jnp.concatenate(terms, axis=0).astype(jnp.bfloat16), select,
+                         preferred_element_type=jnp.float32)
         first_half = lax.broadcasted_iota(jnp.int32, (BLOCK_B, LANES), 1) < LANES // 2
-        for part in range(2):
+        for part in range(TERMS):
             z = spread[part * width:(part + 1) * width]
             plain = [z[:, j * LANES:(j + 1) * LANES] for j in range(reach * tall // LANES)]
             turned = [pltpu.roll(p, LANES // 2, 1) for p in plain]
@@ -196,7 +210,7 @@
             for i in range(reach):
                 low = (c * reach + i) * BLOCK_B
                 table_ref[low:low + BLOCK_B, columns] = joined(
-                    i, [slice(BLOCK_B * k, BLOCK_B * (k + 1)) for k in range(wide)]).astype(jnp.bfloat16)
+                    i, [slice(BLOCK_B * k, BLOCK_B * (k + 1)) for k in range(wide)]).astype(NARROW)
             for e in range(2):
                 if e == 0:
                     lines = [tile_width] + [BLOCK_B * k - 1 for k in range(1, wide)]
@@ -204,8 +218,12 @@
                     lines = [BLOCK_B * (k + 1) for k in range(wide - 1)] + [tile_width + 1]
                 rows = [joined(i, [slice(r, r + 1) for r in lines]) for i in range(reach)]
                 rows.append(jnp.zeros((8 - reach, tall * wide), jnp.float32))
-                low = 2 * reach * BLOCK_B + (c * 2 + e) * 8
-                table_ref[low:low + 8, columns] = jnp.concatenate(rows, axis=0).astype(jnp.bfloat16)
+                extras[part][c].append(jnp.concatenate(rows, axis=0))
+    for part in range(TERMS):
+        columns = slice(part * tall * wide, (part + 1) * tall * wide)
+        low = 2 * reach * BLOCK_B
+        table_ref[low:low + 32, columns] = jnp.concatenate(extras[part][0] + extras[part][1], axis=0).astype(NARROW)
+    return largest * (1.0 / TOP)
 
 
 def gather_nodes(blocks, tile_width, table_ref, nodes_ref):
@@ -215,8 +233,8 @@
     col = cell - row * tile_width
     index = (col // BLOCK_B) * 64 + row // BLOCK_A
     index = index.astype(jnp.float32).astype(jnp.bfloat16)
-    hot = one_hot(narrow_iota((256, index.shape[1]), 0), index)
-    nodes_ref[...] = jnp.dot(table_ref[...], jnp.concatenate([hot, hot], axis=0),
+    hot = one_hot(narrow_iota((256, index.shape[1]), 0), index).astype(NARROW)
+    nodes_ref[...] = jnp.dot(table_ref[...], jnp.concatenate([hot] * TERMS, axis=0),
                              preferred_element_type=jnp.float32)
 
 
@@ -224,7 +242,7 @@
     return jnp.where(diff == -1, weights[0], jnp.where(diff == 0, weights[1], jnp.where(diff == 1, weights[2], 0.0)))
 
 
-def weigh(v, cell, tile_width, nodes, weights_ref):
+def weigh(v, cell, tile_width, nodes, step):
     reach = BLOCK_A + 2
     live = cell >= 0.0
     place = jnp.maximum(cell, 0.0).astype(jnp.int32)
@@ -238,7 +256,7 @@
     bw = banded(lax.broadcasted_iota(jnp.int32, (BLOCK_B, LANES), 0) - col, wb)
     left = jnp.where(col == 0, wb[0], 0.0)
     right = jnp.where(col == BLOCK_B - 1, wb[2], 0.0)
-    scale = jnp.where(live, step_length, 0.0)
+    scale = jnp.where(live, step, 0.0)
     moved = []
     for c in range(2):
         y = None
@@ -255,24 +273,24 @@
     return v + jnp.where(line == 2, moved[0], jnp.where(line == 3, moved[1], 0.0))
 
 
-def advance_block(block, source, at, tile_width, nodes_ref, out_ref, cell_ref):
+def advance_block(block, source, at, tile_width, step, nodes_ref, out_ref, cell_ref):
     for j in range(2):
         lanes = slice(at + j * LANES, at + (j + 1) * LANES)
         v = block[8 * j:8 * j + 8, :]
         cell = block[16 + j:17 + j, :]
         out_ref[:, pl.ds(pl.multiple_of(source * 2 * LANES + j * LANES, LANES), LANES)] = weigh(
-            v, cell, tile_width, lambda rows, lanes=lanes: nodes_ref[rows, lanes], None)
+            v, cell, tile_width, lambda rows, lanes=lanes: nodes_ref[rows, lanes], step)
     cell_ref[pl.ds(source * 2, 2), :] = block[16:18, :].astype(jnp.int32)
 
 
 def exchange_kernel(sizes, width, chunk, part_ref, key_ref, a_ref, b_ref, vel_ref, out_ref, cell_ref,
                     hot_ref, base_ref, pick_ref, low_ref, acc_ref, sorted_ref, cells_ref, first_ref, first_smem,
-                    outgoing, held, edge_ref, halo_ref, table_ref, nodes_even, nodes_odd,
+                    outgoing, held, edge_ref, halo_ref, table_ref, step_ref, nodes_even, nodes_odd,
                     send_sem, recv_sem, halo_send, halo_recv, local_sem, row_sem):
     nx, ny, nz = sizes
     plane = ny * nz
     n = nx * plane
-    group = 16
+    group, ahead = 16, 48
     tile_height, tile_width = vel_ref.shape[1:]
     gx, gy, gz = lax.axis_index("gx"), lax.axis_index("gy"), lax.axis_index("gz")
     column = gy * nz + gz
@@ -367,12 +385,14 @@
             owner = linear(at(*hop(q), 1))
             cut_block(first_smem[0, owner], first_smem[1, owner], sorted_ref, cells_ref, outgoing.at[q])
 
-        @pl.when(p > 0)
+        @pl.when((p > 0) & (p < ahead // 8))
         def _():
             block_copy(p * 8).start()
 
-        for i in range(1, 8):
-            block_copy(p * 8 + i).start()
+        @pl.when(p < ahead // 8)
+        def _():
+            for i in range(1, 8):
+                block_copy(p * 8 + i).start()
         return carry
 
     lax.fori_loop(0, n // 8, dispatch, 0)
@@ -383,7 +403,8 @@
         def _(k=k):
             halo_copy(k, k).wait_recv()
 
-    build_table(vel_ref, halo_ref, table_ref, tile_height, tile_width)
+    unit = build_table(vel_ref, halo_ref, table_ref, tile_height, tile_width)
+    step_ref[...] = jnp.broadcast_to(unit * step_length, step_ref.shape)
 
     def gather(t, nodes_ref):
         gather_nodes([held.at[2 * t], held.at[2 * t + 1]], tile_width, table_ref, nodes_ref)
@@ -391,12 +412,18 @@
     def weigh_pair(t, nodes_ref):
         for i in range(2):
             source = linear(at(*hop(2 * t + i), -1))
-            advance_block(held.at[2 * t + i], source, i * 2 * LANES, tile_width, nodes_ref, out_ref, cell_ref)
+            advance_block(held.at[2 * t + i], source, i * 2 * LANES, tile_width, step_ref[0:1, :],
+                          nodes_ref, out_ref, cell_ref)
 
     arrived(1, 1, 0).wait_recv()
     gather(0, nodes_even)
 
     def one_group(p, carry):
+        @pl.when(p < (n - ahead) // 16)
+        def _():
+            for i in range(16):
+                block_copy(ahead + p * 16 + i).start()
+
         @pl.when(p < n // group - 1)
         def _():
             arrived(p * group + 2, group, p + 1).wait_recv()
@@ -454,7 +481,8 @@
             pltpu.VMEM((owners, 18, LANES), jnp.float32),
             pltpu.VMEM((8, max(tile_height, tile_width)), jnp.float32),
             pltpu.VMEM((8, 8, max(tile_height, tile_width)), jnp.float32),
-            pltpu.VMEM((rows, 2 * 256), jnp.bfloat16),
+            pltpu.VMEM((rows, TERMS * 256), NARROW),
+            pltpu.VMEM((8, LANES), jnp.float32),
             pltpu.VMEM((rows, 4 * LANES), jnp.float32),
             pltpu.VMEM((rows, 4 * LANES), jnp.float32),
             pltpu.SemaphoreType.DMA,

time: 49.9 us -> 47 us (0.942)
  the two profiles are of different devices: /device:TPU:95 before, /device:TPU:1 now
where the time goes in v5:
time: 47 us; the launch traced here: 46.8 us
  Pallas kernels  43.2 us (92%)
  local copies, waits for them, and re-layouts  2.97 us (6%)
  between operations  0.65 us (1%)
    pallas_call x1, Pallas kernels, shards(): pl.pallas_call(functools.partial(exchange_kernel, sizes, width, chunk), o...  43.2 us
    unnamed x4, local copies, waits for them, and re-layouts  2.97 us

profile of v5, /device:TPU:1, one launch (start us, length us, event | category | flops | bytes accessed | tf_op | source)
XLA Modules:
  0.0 46.8 jit_solution(7815055047998500605)
XLA Ops:
  0.6 43.2 %shard_map.68 = (f32[8,32768]{1,0:T(8,128)}, s32[256,128]{1,0:T(8,128)}) custom-call(f32[8,8192]{1,0:T(8,128)} %part_ref.1, s32[1,8192]{1,0:T(1,128)} %bitcast.5, s32[1,8192]{1,0:T(1,128)} %bitcast.6, s32[1,8192]{1,0:T(1,128)} %bitcast.7, f32[2,256,128]{2,1,0:T(8,128)} %vel_ref.1), custom_call_target="tpu_custom_call" | custom-call | tf_op jit(solution)/shard_map/pallas_call | solution.py:464
  43.8 0.0 copy-start
  43.9 2.3 %copy.9 = f32[8,32768]{1,0:T(8,128)} copy(f32[8,32768]{1,0:T(8,128)} %get-tuple-element.8) | data formatting | bytes 2097152
  46.1 0.0 copy-done
  46.2 0.7 %copy.10 = s32[32768]{0:T(1024)} copy(s32[32768]{0:T(1024)S(1)} %bitcast.4) | data formatting | bytes 262144
Async XLA Ops:
  43.8 2.3 %copy-start = (s32[256,128]{1,0:T(8,128)S(1)}, s32[256,128]{1,0:T(8,128)}, u32[]{:S(2)}) copy-start(s32[256,128]{1,0:T(8,128)} %get-tuple-element.5) | copy-start | bytes 393220

commit v6 on v5

--- a/solution.py
+++ b/solution.py
@@ -66,7 +66,7 @@
         return seen, tally
 
     total, tally = lax.fori_loop(0, count // chunk, count_chunk, (
-        jnp.zeros((owners, LANES), jnp.float32), jnp.zeros((owners, LANES), jnp.int32)))
+        jnp.zeros((owners, LANES), jnp.float32), jnp.zeros((owners, LANES), jnp.int32)), unroll=8)
     tally = jnp.sum(tally, axis=1, keepdims=True)
     below = (lax.broadcasted_iota(jnp.int32, (owners, owners), 1)
              < lax.broadcasted_iota(jnp.int32, (owners, owners), 0)).astype(jnp.float32).astype(jnp.bfloat16)
@@ -114,9 +114,9 @@
         return carry
 
     half = count // chunk // 2
-    lax.fori_loop(0, half, place_chunk, 0, unroll=2)
+    lax.fori_loop(0, half, place_chunk, 0, unroll=4)
     aside()
-    lax.fori_loop(half, 2 * half, place_chunk, 0, unroll=2)
+    lax.fori_loop(half, 2 * half, place_chunk, 0, unroll=4)
 
 
 def unpack_sorted(tops, width, tile_width, acc_ref, sorted_ref, cells_ref):
@@ -380,22 +380,22 @@
             halo_ref[k] = jnp.zeros(halo_ref.shape[1:], jnp.float32)
 
     def dispatch(p, carry):
-        for i in range(8):
-            q = p * 8 + i
+        for i in range(16):
+            q = p * 16 + i
             owner = linear(at(*hop(q), 1))
             cut_block(first_smem[0, owner], first_smem[1, owner], sorted_ref, cells_ref, outgoing.at[q])
 
-        @pl.when((p > 0) & (p < ahead // 8))
+        @pl.when((p > 0) & (p < ahead // 16))
         def _():
-            block_copy(p * 8).start()
-
-        @pl.when(p < ahead // 8)
+            block_copy(p * 16).start()
+
+        @pl.when(p < ahead // 16)
         def _():
-            for i in range(1, 8):
-                block_copy(p * 8 + i).start()
+            for i in range(1, 16):
+                block_copy(p * 16 + i).start()
         return carry
 
-    lax.fori_loop(0, n // 8, dispatch, 0)
+    lax.fori_loop(0, n // 16, dispatch, 0)
     held[0] = outgoing[0]
 
     for k in range(8):

time: 47 us -> 42.6 us (0.906)
  Pallas kernels: 43.2 us -> 38.9 us
    pallas_call x1, Pallas kernels: 43.2 us -> 38.9 us  [shards(): pl.pallas_call(functools.partial(exchange_kernel, sizes, width, chunk), o...]
where the time goes in v6:
time: 42.6 us; the launch traced here: 42.5 us
  Pallas kernels  38.9 us (91%)
  local copies, waits for them, and re-layouts  2.97 us (7%)
  between operations  0.65 us (2%)
    pallas_call x1, Pallas kernels, shards(): pl.pallas_call(functools.partial(exchange_kernel, sizes, width, chunk), o...  38.9 us
    unnamed x4, local copies, waits for them, and re-layouts  2.97 us

profile of v6, /device:TPU:1, one launch (start us, length us, event | category | flops | bytes accessed | tf_op | source)
XLA Modules:
  0.0 42.5 jit_solution(16139550841372410071)
XLA Ops:
  0.6 38.9 %shard_map.68 = (f32[8,32768]{1,0:T(8,128)}, s32[256,128]{1,0:T(8,128)}) custom-call(f32[8,8192]{1,0:T(8,128)} %part_ref.1, s32[1,8192]{1,0:T(1,128)} %bitcast.5, s32[1,8192]{1,0:T(1,128)} %bitcast.6, s32[1,8192]{1,0:T(1,128)} %bitcast.7, f32[2,256,128]{2,1,0:T(8,128)} %vel_ref.1), custom_call_target="tpu_custom_call" | custom-call | tf_op jit(solution)/shard_map/pallas_call | solution.py:464
  39.5 0.0 copy-start
  39.5 2.3 %copy.9 = f32[8,32768]{1,0:T(8,128)} copy(f32[8,32768]{1,0:T(8,128)} %get-tuple-element.8) | data formatting | bytes 2097152
  41.8 0.0 copy-done
  41.8 0.7 %copy.10 = s32[32768]{0:T(1024)} copy(s32[32768]{0:T(1024)S(1)} %bitcast.4) | data formatting | bytes 262144
Async XLA Ops:
  39.5 2.3 %copy-start = (s32[256,128]{1,0:T(8,128)S(1)}, s32[256,128]{1,0:T(8,128)}, u32[]{:S(2)}) copy-start(s32[256,128]{1,0:T(8,128)} %get-tuple-element.5) | copy-start | bytes 393220

commit v7 on v6

--- a/solution.py
+++ b/solution.py
@@ -113,10 +113,10 @@
         acc_ref[...] += lax.dot_general(pick_ref[...], low_ref[...], NT, preferred_element_type=jnp.float32)
         return carry
 
-    half = count // chunk // 2
-    lax.fori_loop(0, half, place_chunk, 0, unroll=4)
+    turn = 6
+    lax.fori_loop(0, turn, place_chunk, 0, unroll=6)
     aside()
-    lax.fori_loop(half, 2 * half, place_chunk, 0, unroll=4)
+    lax.fori_loop(turn, count // chunk, place_chunk, 0, unroll=2)
 
 
 def unpack_sorted(tops, width, tile_width, acc_ref, sorted_ref, cells_ref):

time: 42.6 us -> 43 us (level)
  no operation moved by 1% of the time
where the time goes in v7:
time: 43 us; the launch traced here: 42.9 us
  Pallas kernels  39.2 us (91%)
  local copies, waits for them, and re-layouts  2.97 us (7%)
  between operations  0.65 us (2%)
    pallas_call x1, Pallas kernels, shards(): pl.pallas_call(functools.partial(exchange_kernel, sizes, width, chunk), o...  39.2 us
    unnamed x4, local copies, waits for them, and re-layouts  2.97 us

profile of v7, /device:TPU:1, one launch (start us, length us, event | category | flops | bytes accessed | tf_op | source)
XLA Modules:
  0.0 42.9 jit_solution(18173928470968189920)
XLA Ops:
  0.6 39.2 %shard_map.68 = (f32[8,32768]{1,0:T(8,128)}, s32[256,128]{1,0:T(8,128)}) custom-call(f32[8,8192]{1,0:T(8,128)} %part_ref.1, s32[1,8192]{1,0:T(1,128)} %bitcast.5, s32[1,8192]{1,0:T(1,128)} %bitcast.6, s32[1,8192]{1,0:T(1,128)} %bitcast.7, f32[2,256,128]{2,1,0:T(8,128)} %vel_ref.1), custom_call_target="tpu_custom_call" | custom-call | tf_op jit(solution)/shard_map/pallas_call | solution.py:464
  39.9 0.0 copy-start
  39.9 2.3 %copy.9 = f32[8,32768]{1,0:T(8,128)} copy(f32[8,32768]{1,0:T(8,128)} %get-tuple-element.8) | data formatting | bytes 2097152
  42.2 0.0 copy-done
  42.2 0.7 %copy.10 = s32[32768]{0:T(1024)} copy(s32[32768]{0:T(1024)S(1)} %bitcast.4) | data formatting | bytes 262144
Async XLA Ops:
  39.9 2.3 %copy-start = (s32[256,128]{1,0:T(8,128)S(1)}, s32[256,128]{1,0:T(8,128)}, u32[]{:S(2)}) copy-start(s32[256,128]{1,0:T(8,128)} %get-tuple-element.5) | copy-start | bytes 393220
